TPU v7x, 32 devices: a whole 2x2x4 slice. The times are simulated.
32 devices in a mesh: rows: 32 (over z, y, x, core).
Axes of the slice: x: 2, y: 2, z: 4, core: 2. Of those that a mesh axis runs over, the one named last changes fastest.
Arguments:
- source: bfloat16 [65536, 128], P('rows'), may hold values from -6 to 6
- target: bfloat16 [65536, 128], P('rows'), may hold values from -6 to 6
- tile_values: bfloat16 [4096, 128, 128], P('rows'), may hold values from -0.25 to 0.25
- tile_rows: int32 [4096], P('rows'), may hold values from 0 to 15
- tile_peers: int32 [4096], P('rows'), may hold values from 0 to 31
- need_list: int32 [32, 32], P('rows'), may hold values from 0 to 15
- tile_count: int32 [32], P('rows'), may hold values from 1 to 128, as said below
Outputs:
- source_embed: bfloat16 [65536, 128], P('rows')
- target_embed: bfloat16 [65536, 128], P('rows')
Inputs may be any that keep to these rules, and one draw needn't show every extreme that they name: `tile_count`: some device has 128 live tiles; tiles in slots at or past the count take no part.
All inputs are finite; a program needn't handle non-finite values.
Results may differ from a plain program's by a relative error of at most 0.0053.
Values may be sent and summed in bfloat16 or wider, within the bound.
A program may use at most 128 MiB of HBM per device.

v0:
```python
import functools

import jax
import jax.numpy as jnp
from jax import lax
from jax.experimental import pallas as pl
from jax.experimental.pallas import tpu as pltpu
from jax.sharding import PartitionSpec as P

ITERS = 2
UNROLL = 4
epsilon = 1e-06
MESH = pl.DeviceIdType.MESH


def lanes_for(count):
    return -(-count // 128) * 128


def index_along(shape, axis):
    return lax.broadcasted_iota(jnp.int32, shape, axis).astype(jnp.float32)


def place_groups(keys, groups, per_slot, slots, out, seat_row, last_row):
    items, lanes = keys.shape[1], lanes_for(groups)
    key = jnp.broadcast_to(keys, (items, items))
    key_down = jnp.broadcast_to(keys, (lanes_for(items), items)).T
    before = (key_down[:, :items] == key) & (
        index_along((items, items), 1) < index_along((items, items), 0)
    )
    rank = jnp.sum(before.astype(jnp.float32), axis=1, keepdims=True)
    lane = index_along((items, lanes), 1)
    member = (jnp.broadcast_to(key_down[:, :1], (items, lanes)) == lane).astype(jnp.float32)
    count = jnp.sum(member, axis=0, keepdims=True)
    used = jnp.floor((count + (per_slot - 1)) * (1.0 / per_slot))
    used_down = jnp.broadcast_to(used, (lanes, lanes)).T
    earlier = (index_along((lanes, lanes), 0) < index_along((lanes, lanes), 1)).astype(jnp.float32)
    start = jnp.sum(used_down * earlier, axis=0, keepdims=True)
    last = jnp.where(used > 0, start + used - 1, float(slots))
    first = jnp.sum(member * start, axis=1, keepdims=True)
    place = jnp.where(key_down[:, :1] >= 0, per_slot * first + rank, -1.0)
    seats = lanes_for(slots * per_slot)
    for chunk in range(seats // 128):
        hot = jnp.broadcast_to(place, (items, 128)) == index_along((items, 128), 1) + 128 * chunk
        item = jnp.where(hot, index_along((items, 128), 0) - items, 0.0)
        chosen = items + jnp.sum(item, axis=0, keepdims=True)
        out[pl.ds(seat_row + chunk, 1), :] = chosen.astype(jnp.int32)
    for chunk in range(lanes // 128):
        out[pl.ds(last_row + chunk, 1), :] = last[:, 128 * chunk : 128 * (chunk + 1)].astype(
            jnp.int32
        )


def slots_for(items, groups):
    pairs = (items + min(items, groups)) // 2
    return -(-pairs // UNROLL) * UNROLL


def kernel(
    n,
    f_slots,
    b_slots,
    row_of,
    peer_of,
    live_count,
    rows_lane,
    peers_lane,
    need,
    source_hbm,
    target_hbm,
    tiles_hbm,
    source_out,
    target_out,
    x_out,
    x_ins,
    y_out,
    y_ins,
    x_now,
    y_now,
    y_base,
    f_sums,
    b_sums,
    c_sums,
    source,
    target,
    tiles,
    need_all,
    need_at,
    tile_plan,
    tile_at,
    part_plan,
    part_at,
    send_sem,
    recv_sem,
    need_send,
    need_recv,
    load_sem,
):
    me = lax.axis_index("rows")
    rows, side, width = source.shape
    tile_total = tiles_hbm.shape[0]
    f_seat, f_last = 0, lanes_for(2 * f_slots) // 128
    b_seat = f_last + lanes_for(rows) // 128
    b_last = b_seat + lanes_for(2 * b_slots) // 128
    c_last = lanes_for(n) // 128

    barrier = pltpu.get_barrier_semaphore()

    def greet(k, carry):
        pl.semaphore_signal(
            barrier, inc=1, device_id=(lax.rem(me + k, n),), device_id_type=MESH
        )
        return carry

    lax.fori_loop(1, n, greet, 0)
    source_load = pltpu.make_async_copy(source_hbm, source, load_sem.at[5])
    source_load.start()
    target_load = pltpu.make_async_copy(target_hbm, target, load_sem.at[0])
    target_load.start()
    tile_load = pltpu.make_async_copy(tiles_hbm, tiles.at[pl.ds(0, tile_total)], load_sem.at[1])
    tile_load.start()

    zero_block = jnp.zeros((side, width), jnp.bfloat16)
    zero_sum = jnp.zeros((side, width), jnp.float32)
    tiles[tile_total] = jnp.zeros((side, side), jnp.bfloat16)
    f_sums[f_slots] = zero_sum
    b_sums[b_slots] = zero_block
    c_sums[n] = zero_sum
    need_all[me] = need[...]
    pl.semaphore_wait(barrier, n - 1)

    def ask(k, carry):
        pltpu.make_async_remote_copy(
            src_ref=need,
            dst_ref=need_all.at[me],
            send_sem=need_send.at[0],
            recv_sem=need_recv.at[0],
            device_id=(lax.rem(me + k, n),),
            device_id_type=MESH,
        ).start()
        return carry

    lax.fori_loop(1, n, ask, 0)

    def turn(b, carry):
        flipped = target[b].astype(jnp.float32).T
        y_base[b] = flipped
        y_now[b] = flipped.astype(jnp.bfloat16)
        return carry

    def plan_tiles():
        live = lax.broadcasted_iota(jnp.int32, (1, tile_total), 1) < live_count[0]
        row_keys = jnp.where(live, rows_lane[...], -1).astype(jnp.float32)
        peer_keys = jnp.where(live, peers_lane[...], -1).astype(jnp.float32)
        place_groups(row_keys, rows, 2, f_slots, tile_plan, f_seat, f_last)
        place_groups(peer_keys, n, 2, b_slots, tile_plan, b_seat, b_last)
        load = pltpu.make_async_copy(tile_plan, tile_at, load_sem.at[3])
        load.start()
        load.wait()

    def plan_parts():
        table = need_all[...].reshape(n, need_all.shape[2]).astype(jnp.float32)
        mine = index_along(table.shape, 1) == me.astype(jnp.float32)
        wanted = jnp.sum(jnp.where(mine, table, 0.0), axis=1, keepdims=True)
        keys = jnp.broadcast_to(wanted, (n, 128)).T[:1]
        place_groups(keys, rows, 1, n, part_plan, 0, c_last)
        load = pltpu.make_async_copy(part_plan, part_at, load_sem.at[4])
        load.start()
        load.wait()

    def seat(table, first, index, top):
        return jnp.clip(table[first + index // 128, index % 128], 0, top)

    def tile_pair(first, q):
        left = seat(tile_at, first, 2 * q, tile_total)
        right = seat(tile_at, first, 2 * q + 1, tile_total)
        return left, right, jnp.minimum(left, tile_total - 1), jnp.minimum(right, tile_total - 1)

    def asked(d):
        return jnp.clip(need_at[d, 0, me], 0, rows - 1)

    def send(out, inn, phase, it, fill):
        def one(k, carry):
            peer = lax.rem(me + k, n)
            out[it, peer] = fill(peer)
            pltpu.make_async_remote_copy(
                src_ref=out.at[it, peer],
                dst_ref=inn.at[me],
                send_sem=send_sem.at[phase],
                recv_sem=recv_sem.at[phase],
                device_id=(peer,),
                device_id_type=MESH,
            ).start()
            return carry

        lax.fori_loop(1, n, one, 0)
        inn[me] = fill(me)

    def all_of(buffer, sem):
        view = buffer.at[pl.ds(0, n - 1)]
        pltpu.make_async_copy(view, view, sem).wait()

    def send_x(blocks, it):
        send(x_out, x_ins[it], 2 * it, it, lambda p: blocks[asked(p)])

    def backward(it):
        def one(q, carry):
            total, key = carry
            left, right, left_at, right_at = tile_pair(b_seat, q)
            flipped = jnp.concatenate([y_now[row_of[left_at]], y_now[row_of[right_at]]], axis=1)
            stack = jnp.concatenate([tiles[left], tiles[right]], axis=0)
            product = jnp.dot(flipped, stack, preferred_element_type=jnp.float32)
            new_key = peer_of[left_at]
            total = total * (new_key == key).astype(jnp.float32) + product
            b_sums[q] = total.astype(jnp.bfloat16)
            return total, new_key

        lax.fori_loop(0, b_slots, one, (zero_sum, jnp.int32(-1)), unroll=UNROLL)
        send(y_out, y_ins[it], 2 * it + 1, it, lambda p: b_sums[seat(tile_at, b_last, p, b_slots)])

    def forward(it, result):
        x_in = x_ins[it]
        all_of(x_in, recv_sem.at[2 * it])

        def one(q, carry):
            total, key = carry
            left, right, left_at, right_at = tile_pair(f_seat, q)
            stack = jnp.concatenate([tiles[left], tiles[right]], axis=1)
            blocks = jnp.concatenate([x_in[peer_of[left_at]], x_in[peer_of[right_at]]], axis=0)
            product = jnp.dot(stack, blocks, preferred_element_type=jnp.float32)
            new_key = row_of[left_at]
            total = total * (new_key == key).astype(jnp.float32) + product
            f_sums[q] = total
            return total, new_key

        lax.fori_loop(0, f_slots, one, (zero_sum, jnp.int32(-1)), unroll=UNROLL)

        def settle(b, carry):
            total = source[b].astype(jnp.float32) + f_sums[seat(tile_at, f_last, b, f_slots)]
            scale = lax.rsqrt(jnp.mean(total * total, axis=-1, keepdims=True) + epsilon)
            result[b] = (total * scale).astype(jnp.bfloat16)
            return carry

        lax.fori_loop(0, rows, settle, 0)

    def combine(it, final):
        y_in = y_ins[it]
        all_of(y_in, recv_sem.at[2 * it + 1])

        def one(k, carry):
            total, key = carry
            sender = seat(part_at, 0, k, n - 1)
            new_key = asked(sender)
            total = total * (new_key == key).astype(jnp.float32) + y_in[sender].astype(jnp.float32)
            c_sums[k] = total
            return total, new_key

        lax.fori_loop(0, n, one, (zero_sum, jnp.int32(-1)), unroll=UNROLL)

        def settle(b, carry):
            total = y_base[b] + c_sums[seat(part_at, c_last, b, n)]
            scale = lax.rsqrt(jnp.mean(total * total, axis=0, keepdims=True) + epsilon)
            if final:
                target_out[b] = (total * scale).T.astype(jnp.bfloat16)
            else:
                y_now[b] = (total * scale).astype(jnp.bfloat16)
            return carry

        lax.fori_loop(0, rows, settle, 0)

    all_of(need_all, need_recv.at[0])
    need_load = pltpu.make_async_copy(need_all, need_at, load_sem.at[2])
    need_load.start()
    need_load.wait()
    source_load.wait()
    send_x(source, 0)
    plan_tiles()
    target_load.wait()
    lax.fori_loop(0, rows, turn, 0)
    tile_load.wait()
    backward(0)
    plan_parts()
    for it in range(ITERS):
        final = it == ITERS - 1
        forward(it, source_out if final else x_now)
        if not final:
            send_x(x_now, it + 1)
        combine(it, final)
        if not final:
            backward(it + 1)
    all_of(need_all, need_send.at[0])
    for it in range(ITERS):
        all_of(x_out.at[it], send_sem.at[2 * it])
        all_of(y_out.at[it], send_sem.at[2 * it + 1])


def shards(source, target, tile_values, tile_rows, tile_peers, need_list, tile_count):
    n = lax.axis_size("rows")
    tiles_here, side, _ = tile_values.shape
    width = source.shape[1]
    rows = source.shape[0] // side
    f_slots = slots_for(tiles_here, rows)
    b_slots = slots_for(tiles_here, n)
    tile_plan = (
        lanes_for(2 * f_slots) + lanes_for(rows) + lanes_for(2 * b_slots) + lanes_for(n)
    ) // 128
    part_plan = (lanes_for(n) + lanes_for(rows)) // 128
    block = (side, width)
    vmem = pl.BlockSpec(memory_space=pltpu.VMEM)
    smem = pl.BlockSpec(memory_space=pltpu.SMEM)
    source_now, target_now = pl.pallas_call(
        functools.partial(kernel, n, f_slots, b_slots),
        out_shape=[jax.ShapeDtypeStruct((rows,) + block, jnp.bfloat16)] * 2,
        in_specs=[smem] * 3 + [vmem] * 3 + [pl.BlockSpec(memory_space=pltpu.HBM)] * 3,
        out_specs=[vmem, vmem],
        scratch_shapes=[
            pltpu.VMEM((ITERS, n) + block, jnp.bfloat16),
            [pltpu.VMEM((n,) + block, jnp.bfloat16)] * ITERS,
            pltpu.VMEM((ITERS, n) + block, jnp.bfloat16),
            [pltpu.VMEM((n,) + block, jnp.bfloat16)] * ITERS,
            pltpu.VMEM((rows,) + block, jnp.bfloat16),
            pltpu.VMEM((rows,) + block, jnp.bfloat16),
            pltpu.VMEM((rows,) + block, jnp.float32),
            pltpu.VMEM((f_slots + 1,) + block, jnp.float32),
            pltpu.VMEM((b_slots + 1,) + block, jnp.bfloat16),
            pltpu.VMEM((n + 1,) + block, jnp.float32),
            pltpu.VMEM((rows,) + block, jnp.bfloat16),
            pltpu.VMEM((rows,) + block, jnp.bfloat16),
            pltpu.VMEM((tiles_here + 1, side, side), jnp.bfloat16),
            pltpu.VMEM((n, 1, n), jnp.int32),
            pltpu.SMEM((n, 1, n), jnp.int32),
            pltpu.VMEM((tile_plan, 128), jnp.int32),
            pltpu.SMEM((tile_plan, 128), jnp.int32),
            pltpu.VMEM((part_plan, 128), jnp.int32),
            pltpu.SMEM((part_plan, 128), jnp.int32),
            pltpu.SemaphoreType.DMA((2 * ITERS,)),
            pltpu.SemaphoreType.DMA((2 * ITERS,)),
            pltpu.SemaphoreType.DMA((1,)),
            pltpu.SemaphoreType.DMA((1,)),
            pltpu.SemaphoreType.DMA((6,)),
        ],
        compiler_params=pltpu.CompilerParams(
            collective_id=0, has_side_effects=True, vmem_limit_bytes=67043328
        ),
    )(
        tile_rows,
        tile_peers,
        tile_count,
        tile_rows.reshape(1, -1),
        tile_peers.reshape(1, -1),
        need_list,
        source.reshape((rows,) + block),
        target.reshape((rows,) + block),
        tile_values,
    )
    return source_now.reshape(-1, width), target_now.reshape(-1, width)


def solution(mesh):
    return jax.shard_map(
        shards,
        mesh=mesh,
        in_specs=(
            P("rows", None),
            P("rows", None),
            P("rows", None, None),
            P("rows"),
            P("rows"),
            P("rows", None),
            P("rows"),
        ),
        out_specs=(P("rows", None), P("rows", None)),
        check_vma=False,
    )
```

profile of v0, /device:TPU:13, one launch (start us, length us, event | category | flops | bytes accessed | tf_op | source)
XLA Modules:
  0.0 111.2 jit_solution(779150285730979547)
XLA Ops:
  1.3 106.2 %shard_map.86 = (bf16[16,128,128]{2,1,0:T(8,128)(2,1)}, bf16[16,128,128]{2,1,0:T(8,128)(2,1)}) custom-call(s32[128]{0:T(128)} %row_of.1, s32[128]{0:T(128)} %peer_of.1, s32[1]{0:T(128)S(6)} %copy.11.live_count, s32[1,128]{1,0:T(1,128)} %bitcast.10, s32[1,128]{1,0:T(1,128)} %bitcast.11, s32[1,32]{1,0:T(1,128)} %need.1, bf16[16,128,128]{2,1,0:T(8,128)(2,1)} %bitcast.8, ...), custom_call_target="tpu_custom_call" | custom-call | tf_op jit(solution)/shard_map/pallas_call | solution.py:311
  107.5 1.9 %copy.12 = bf16[2048,128]{1,0:T(8,128)(2,1)} copy(bf16[2048,128]{1,0:T(8,128)(2,1)} %bitcast.7) | data formatting | bytes 1048576
  109.4 1.9 %copy.13 = bf16[2048,128]{1,0:T(8,128)(2,1)} copy(bf16[2048,128]{1,0:T(8,128)(2,1)} %bitcast.6) | data formatting | bytes 1048576
where the time goes:
time: 111 us
  Pallas kernels  106 us (95%)
  local copies, waits for them, and re-layouts  3.74 us (3%)
  between operations  1.29 us (1%)
    pallas_call x1, Pallas kernels, shards(): pl.pallas_call(functools.partial(kernel, n, f_slots, b_slots), out_shape=...  106 us
    unnamed x2, local copies, waits for them, and re-layouts  3.74 us

commit v1 on v0

--- a/solution.py
+++ b/solution.py
@@ -310,7 +310,7 @@
     smem = pl.BlockSpec(memory_space=pltpu.SMEM)
     source_now, target_now = pl.pallas_call(
         functools.partial(kernel, n, f_slots, b_slots),
-        out_shape=[jax.ShapeDtypeStruct((rows,) + block, jnp.bfloat16)] * 2,
+        out_shape=[pltpu.VMEM((rows,) + block, jnp.bfloat16)] * 2,
         in_specs=[smem] * 3 + [vmem] * 3 + [pl.BlockSpec(memory_space=pltpu.HBM)] * 3,
         out_specs=[vmem, vmem],
         scratch_shapes=[
@@ -340,7 +340,7 @@
             pltpu.SemaphoreType.DMA((6,)),
         ],
         compiler_params=pltpu.CompilerParams(
-            collective_id=0, has_side_effects=True, vmem_limit_bytes=67043328
+            collective_id=0, has_side_effects=True, vmem_limit_bytes=60000000
         ),
     )(
         tile_rows,

time: 111 us -> 108 us (0.973)
  local copies, waits for them, and re-layouts: 3.74 us -> 1.59 us
    unnamed x2, local copies, waits for them, and re-layouts: 3.74 us -> 1.59 us
where the time goes in v1:
time: 108 us
  Pallas kernels  105 us (97%)
  local copies, waits for them, and re-layouts  1.59 us (1%)
  between operations  1.29 us (1%)
    pallas_call x1, Pallas kernels, shards(): pl.pallas_call(functools.partial(kernel, n, f_slots, b_slots), out_shape=...  105 us

profile of v1, /device:TPU:13, one launch (start us, length us, event | category | flops | bytes accessed | tf_op | source)
XLA Modules:
  0.0 108.1 jit_solution(15866656413967279743)
XLA Ops:
  1.3 105.2 %shard_map.86 = (bf16[16,128,128]{2,1,0:T(8,128)(2,1)S(1)}, bf16[16,128,128]{2,1,0:T(8,128)(2,1)S(1)}) custom-call(s32[128]{0:T(128)} %row_of.1, s32[128]{0:T(128)} %peer_of.1, s32[1]{0:T(128)S(6)} %copy.13.live_count, s32[1,128]{1,0:T(1,128)} %bitcast.10, s32[1,128]{1,0:T(1,128)} %bitcast.11, s32[1,32]{1,0:T(1,128)} %need.1, bf16[16,128,128]{2,1,0:T(8,128)(2,1)} %bitcast.8, ...), custom_call_target="tpu_custom_call" | custom-call | tf_op jit(solution)/shard_map/pallas_call | solution.py:311
  106.5 0.8 copy.11
  107.3 0.8 copy.12

commit v2 on v1

--- a/solution.py
+++ b/solution.py
@@ -56,7 +56,14 @@
     return -(-pairs // UNROLL) * UNROLL
 
 
-def kernel(
+def read_peers(peer_keys, lanes):
+    items = peer_keys.shape[1]
+    key_down = jnp.broadcast_to(peer_keys, (lanes_for(items), items)).T
+    member = jnp.broadcast_to(key_down[:, :1], (items, lanes)) == index_along((items, lanes), 1)
+    return jnp.sum(member.astype(jnp.float32), axis=0, keepdims=True)
+
+
+def general(
     n,
     f_slots,
     b_slots,
@@ -294,7 +301,517 @@
         all_of(y_out.at[it], send_sem.at[2 * it + 1])
 
 
-def shards(source, target, tile_values, tile_rows, tile_peers, need_list, tile_count):
+def fast(
+    n,
+    cap,
+    f_slots,
+    b_slots,
+    row_of,
+    peer_of,
+    live_count,
+    rows_lane,
+    peers_lane,
+    need,
+    source_hbm,
+    target_hbm,
+    tiles_hbm,
+    source_out,
+    target_out,
+    over_out,
+    x_near_out,
+    x_far_out,
+    x_ins,
+    gates,
+    relay_out,
+    y_out,
+    y_near_ins,
+    y_gates,
+    y_cross_out,
+    y_far_ins,
+    x_now,
+    y_now,
+    y_base,
+    y_mid,
+    f_sums,
+    b_sums,
+    c_sums,
+    source,
+    target,
+    tiles,
+    need_mine,
+    need_all,
+    need_at,
+    tile_plan,
+    tile_at,
+    part_plan,
+    part_at,
+    far_plan,
+    far_at,
+    x_send,
+    x_recv,
+    gate_send,
+    gate_recv,
+    relay_send,
+    y_send,
+    y_near_recv,
+    y_gate_recv,
+    y_cross_send,
+    y_far_recv,
+    need_send,
+    need_recv,
+    load_sem,
+):
+    me = lax.axis_index("rows")
+    rows, side, width = source.shape
+    tile_total = tiles_hbm.shape[0]
+    lanes = lanes_for(n)
+    half, plane = n // 2, n // 4
+    upper = me // half
+    near_first, far_first = upper * half, (1 - upper) * half
+    spot, column = me % half, me % plane
+    inner = me // plane == 1 + upper
+    outer = jnp.logical_not(inner)
+    far_gate = (2 - upper) * plane + column
+    near_gates = (1 + upper) * plane
+    far_planes = (3 * (1 - upper) * plane, (2 - upper) * plane)
+    far_owner = tuple(first + column for first in far_planes)
+    f_seat, f_last = 0, lanes_for(2 * f_slots) // 128
+    b_seat = f_last + lanes_for(rows) // 128
+    b_last = b_seat + lanes_for(2 * b_slots) // 128
+    c_last = lanes_for(n) // 128
+    part_rows = c_last + lanes_for(rows) // 128
+    far_list = n
+    far_slot = n + rows
+
+    barrier = pltpu.get_barrier_semaphore()
+
+    def greet(k, carry):
+        pl.semaphore_signal(
+            barrier, inc=1, device_id=(lax.rem(me + k, n),), device_id_type=MESH
+        )
+        return carry
+
+    lax.fori_loop(1, n, greet, 0)
+    source_load = pltpu.make_async_copy(source_hbm, source, load_sem.at[5])
+    source_load.start()
+    target_load = pltpu.make_async_copy(target_hbm, target, load_sem.at[0])
+    target_load.start()
+    tile_load = pltpu.make_async_copy(tiles_hbm, tiles.at[pl.ds(0, tile_total)], load_sem.at[1])
+    tile_load.start()
+
+    live = lax.broadcasted_iota(jnp.int32, (1, tile_total), 1) < live_count[0]
+    row_keys = jnp.where(live, rows_lane[...], -1).astype(jnp.float32)
+    peer_keys = jnp.where(live, peers_lane[...], -1).astype(jnp.float32)
+    read = read_peers(peer_keys, lanes)
+    need_mine[...] = jnp.full((1, lanes), -1, jnp.int32)
+    need_mine[:, :n] = jnp.where(read[:, :n] > 0, need[...], -1)
+    zero_block = jnp.zeros((side, width), jnp.bfloat16)
+    zero_sum = jnp.zeros((side, width), jnp.float32)
+    tiles[tile_total] = jnp.zeros((side, side), jnp.bfloat16)
+    f_sums[f_slots] = zero_sum
+    b_sums[b_slots] = zero_block
+    c_sums[half] = zero_sum
+    for it in range(ITERS):
+        y_far_ins[it][cap] = zero_block
+    need_all[me] = need_mine[...]
+    def turn(b, carry):
+        flipped = target[b].astype(jnp.float32).T
+        y_base[b] = flipped
+        y_now[b] = flipped.astype(jnp.bfloat16)
+        return carry
+
+    def plan_tiles():
+        place_groups(row_keys, rows, 2, f_slots, tile_plan, f_seat, f_last)
+        place_groups(peer_keys, n, 2, b_slots, tile_plan, b_seat, b_last)
+        load = pltpu.make_async_copy(tile_plan, tile_at, load_sem.at[3])
+        load.start()
+        load.wait()
+
+    plan_tiles()
+    target_load.wait()
+    lax.fori_loop(0, rows, turn, 0)
+    source_load.wait()
+    pl.semaphore_wait(barrier, n - 1)
+
+    def push(src, dst, send_sem, recv_sem, peer):
+        pltpu.make_async_remote_copy(
+            src_ref=src,
+            dst_ref=dst,
+            send_sem=send_sem,
+            recv_sem=recv_sem,
+            device_id=(peer,),
+            device_id_type=MESH,
+        ).start()
+
+    def all_of(buffer, count, sem):
+        view = buffer.at[pl.ds(0, count)]
+        pltpu.make_async_copy(view, view, sem).wait()
+
+    def ask(k, carry):
+        peer = lax.rem(me + k, n)
+        push(need_mine, need_all.at[me], need_send.at[0], need_recv.at[0], peer)
+        return carry
+
+    lax.fori_loop(1, n, ask, 0)
+
+    def send_whole(s, first, count):
+        push(
+            source.at[pl.ds(first, count)],
+            gates[0][s].at[pl.ds(first, count)],
+            gate_send.at[0],
+            gate_recv.at[s],
+            far_gate,
+        )
+
+    def needs():
+        return need_all[...].reshape(n, lanes).astype(jnp.float32)
+
+    def plan_far():
+        table = needs()
+        early = index_along((1, lanes), 1) < half
+        before = jnp.zeros((1, lanes), jnp.float32)
+        place = jnp.zeros((n, lanes), jnp.float32)
+        listed = jnp.zeros((rows, lanes), jnp.float32)
+        for b in range(rows):
+            hit = (table == b).astype(jnp.float32)
+            low = jnp.max(hit[:half], axis=0, keepdims=True)
+            high = jnp.max(hit[half:], axis=0, keepdims=True)
+            used = jnp.where(early, high, low)
+            place = place + hit * before
+            chosen = jnp.where(used > 0, before, -1.0)
+            listed = jnp.where(index_along((rows, lanes), 0) == chosen, float(b), listed)
+            far_plan[pl.ds(far_slot + b, 1), :] = jnp.where(used > 0, before, float(cap)).astype(
+                jnp.int32
+            )
+            before = before + used
+        far_plan[pl.ds(0, n), :] = place.astype(jnp.int32)
+        far_plan[pl.ds(far_list, rows), :] = listed.astype(jnp.int32)
+        worst = jnp.max(before, axis=1, keepdims=True)
+        over_out[...] = (worst > cap).astype(jnp.int32)
+        load = pltpu.make_async_copy(far_plan, far_at, load_sem.at[6])
+        load.start()
+        load.wait()
+
+    def plan_parts():
+        table = needs()
+        sender = index_along((n, lanes), 0)
+        lane = index_along((n, lanes), 1)
+        near = (sender >= near_first.astype(jnp.float32)) & (
+            sender < (near_first + half).astype(jnp.float32)
+        )
+        known = near & (table >= 0)
+        place = far_plan[pl.ds(0, n), :].astype(jnp.float32)
+
+        def column_of(values, at):
+            mine = lane == at.astype(jnp.float32)
+            column = jnp.sum(jnp.where(mine, values, 0.0), axis=1, keepdims=True)
+            return jnp.broadcast_to(column, (n, 128)).T[:1]
+
+        def plan(values, at, first):
+            keys = column_of(jnp.where(known, values, -1.0), at)
+            place_groups(keys, rows, 1, half, part_plan, first, first + c_last)
+
+        plan(table, me, 0)
+        for s in range(2):
+            plan(place, far_owner[s], (1 + s) * part_rows)
+        load = pltpu.make_async_copy(part_plan, part_at, load_sem.at[4])
+        load.start()
+        load.wait()
+
+    def seat(table, first, index, top):
+        return jnp.clip(table[first + index // 128, index % 128], 0, top)
+
+    def tile_pair(first, q):
+        left = seat(tile_at, first, 2 * q, tile_total)
+        right = seat(tile_at, first, 2 * q + 1, tile_total)
+        return left, right, jnp.minimum(left, tile_total - 1), jnp.minimum(right, tile_total - 1)
+
+    def asked(d):
+        return jnp.clip(need_at[d, 0, me], 0, rows - 1)
+
+    def send_near(blocks, it):
+        x_in = x_ins[it]
+        if it:
+            all_of(x_in, half - 1, x_send.at[it - 1])
+
+        def one(k, carry):
+            peer = near_first + lax.rem(spot + k, half)
+            x_near_out[k] = blocks[asked(peer)]
+            push(x_near_out.at[k], x_in.at[me], x_send.at[it], x_recv.at[it], peer)
+            return carry
+
+        lax.fori_loop(1, half, one, 0)
+        x_in[me] = blocks[asked(me)]
+
+    def send_far(blocks, it, s):
+        def one(i, carry):
+            x_far_out[i] = blocks[jnp.clip(far_at[far_list + i, me], 0, rows - 1)]
+            return carry
+
+        lax.fori_loop(0, cap, one, 0)
+        push(
+            x_far_out,
+            gates[it][s].at[pl.ds(0, cap)],
+            gate_send.at[it],
+            gate_recv.at[2 * it + s],
+            far_gate,
+        )
+
+    def relay(it, s, whole):
+        gate, x_in, owner = gates[it][s], x_ins[it], far_owner[s]
+        if it:
+            all_of(x_in, half - 1, relay_send.at[2 * (it - 1) + s])
+        all_of(gate, rows if whole else cap, gate_recv.at[2 * it + s])
+
+        def block(d):
+            at = need_at[d, 0, owner] if whole else far_at[d, owner]
+            return gate[jnp.clip(at, 0, (rows if whole else cap) - 1)]
+
+        def one(k, carry):
+            peer = near_first + lax.rem(spot + k, half)
+            relay_out[s, k] = block(peer)
+            push(
+                relay_out.at[s, k],
+                x_in.at[owner],
+                relay_send.at[2 * it + s],
+                x_recv.at[it],
+                peer,
+            )
+            return carry
+
+        lax.fori_loop(1, half, one, 0)
+        x_in[owner] = block(me)
+
+    def backward(it):
+        def one(q, carry):
+            total, key = carry
+            left, right, left_at, right_at = tile_pair(b_seat, q)
+            flipped = jnp.concatenate([y_now[row_of[left_at]], y_now[row_of[right_at]]], axis=1)
+            stack = jnp.concatenate([tiles[left], tiles[right]], axis=0)
+            product = jnp.dot(flipped, stack, preferred_element_type=jnp.float32)
+            new_key = peer_of[left_at]
+            total = total * (new_key == key).astype(jnp.float32) + product
+            b_sums[q] = total.astype(jnp.bfloat16)
+            return total, new_key
+
+        lax.fori_loop(0, b_slots, one, (zero_sum, jnp.int32(-1)), unroll=UNROLL)
+
+    def part(peer):
+        return b_sums[seat(tile_at, b_last, peer, b_slots)]
+
+    def send_parts(it, s):
+        gate_in = y_gates[it][s]
+
+        def one(k, carry):
+            gate = lax.rem(column + k, plane)
+            peer = far_planes[s] + gate
+            y_out[peer] = part(peer)
+            push(
+                y_out.at[peer],
+                gate_in.at[spot],
+                y_send.at[it],
+                y_gate_recv.at[2 * it + s],
+                near_gates + gate,
+            )
+            return carry
+
+        @pl.when(outer)
+        def _():
+            one(0, 0)
+
+        @pl.when(inner)
+        def _():
+            gate_in[spot] = part(far_owner[s])
+
+        lax.fori_loop(1, plane, one, 0)
+
+    def send_near_parts(it):
+        def one(k, carry):
+            peer = near_first + lax.rem(spot + k, half)
+            y_out[peer] = part(peer)
+            push(y_out.at[peer], y_near_ins[it].at[spot], y_send.at[it], y_near_recv.at[it], peer)
+            return carry
+
+        lax.fori_loop(1, half, one, 0)
+        y_near_ins[it][spot] = part(me)
+
+    def sent_parts(it):
+        @pl.when(inner)
+        def _():
+            all_of(y_out, n - 3, y_send.at[it])
+
+        @pl.when(outer)
+        def _():
+            all_of(y_out, n - 1, y_send.at[it])
+
+    def forward(it, result):
+        x_in = x_ins[it]
+
+        @pl.when(inner)
+        def _():
+            all_of(x_in, n - 3, x_recv.at[it])
+
+        @pl.when(outer)
+        def _():
+            all_of(x_in, n - 1, x_recv.at[it])
+
+        def one(q, carry):
+            total, key = carry
+            left, right, left_at, right_at = tile_pair(f_seat, q)
+            stack = jnp.concatenate([tiles[left], tiles[right]], axis=1)
+            blocks = jnp.concatenate([x_in[peer_of[left_at]], x_in[peer_of[right_at]]], axis=0)
+            product = jnp.dot(stack, blocks, preferred_element_type=jnp.float32)
+            new_key = row_of[left_at]
+            total = total * (new_key == key).astype(jnp.float32) + product
+            f_sums[q] = total
+            return total, new_key
+
+        lax.fori_loop(0, f_slots, one, (zero_sum, jnp.int32(-1)), unroll=UNROLL)
+
+        def settle(b, carry):
+            total = source[b].astype(jnp.float32) + f_sums[seat(tile_at, f_last, b, f_slots)]
+            scale = lax.rsqrt(jnp.mean(total * total, axis=-1, keepdims=True) + epsilon)
+            result[b] = (total * scale).astype(jnp.bfloat16)
+            return carry
+
+        lax.fori_loop(0, rows, settle, 0)
+
+    def gather(y_in, first, key_of):
+        def one(k, carry):
+            total, key = carry
+            sender = seat(part_at, first, k, n - 1)
+            new_key = key_of(sender)
+            at = jnp.clip(sender - near_first, 0, half - 1)
+            total = total * (new_key == key).astype(jnp.float32) + y_in[at].astype(jnp.float32)
+            c_sums[k] = total
+            return total, new_key
+
+        lax.fori_loop(0, half, one, (zero_sum, jnp.int32(-1)), unroll=UNROLL)
+
+    def cross_y(it, s):
+        first = (1 + s) * part_rows
+        all_of(y_gates[it][s], half - 1, y_gate_recv.at[2 * it + s])
+        gather(y_gates[it][s], first, lambda d: far_at[d, far_owner[s]])
+        if it:
+            all_of(y_cross_out.at[s], cap, y_cross_send.at[2 * (it - 1) + s])
+
+        def one(i, carry):
+            total = c_sums[seat(part_at, first + c_last, i, half)]
+            y_cross_out[s, i] = total.astype(jnp.bfloat16)
+            return carry
+
+        lax.fori_loop(0, cap, one, 0)
+        push(
+            y_cross_out.at[s],
+            y_far_ins[it].at[pl.ds(0, cap)],
+            y_cross_send.at[2 * it + s],
+            y_far_recv.at[it],
+            far_owner[s],
+        )
+
+    def combine_near(it):
+        all_of(y_near_ins[it], half - 1, y_near_recv.at[it])
+        gather(y_near_ins[it], 0, asked)
+
+        def settle(b, carry):
+            y_mid[b] = y_base[b] + c_sums[seat(part_at, c_last, b, half)]
+            return carry
+
+        lax.fori_loop(0, rows, settle, 0)
+
+    def combine_far(it, final):
+        y_far = y_far_ins[it]
+        all_of(y_far, cap, y_far_recv.at[it])
+
+        def settle(b, carry):
+            at = jnp.clip(far_at[far_slot + b, me], 0, cap)
+            total = y_mid[b] + y_far[at].astype(jnp.float32)
+            scale = lax.rsqrt(jnp.mean(total * total, axis=0, keepdims=True) + epsilon)
+            if final:
+                target_out[b] = (total * scale).T.astype(jnp.bfloat16)
+            else:
+                y_now[b] = (total * scale).astype(jnp.bfloat16)
+            return carry
+
+        lax.fori_loop(0, rows, settle, 0)
+
+    first_part = 5 * rows // 8
+
+    @pl.when(outer)
+    def _():
+        send_whole(0, 0, first_part)
+
+    @pl.when(inner)
+    def _():
+        send_whole(1, 0, rows)
+
+    tile_load.wait()
+    backward(0)
+    send_parts(0, 1)
+
+    @pl.when(outer)
+    def _():
+        send_whole(0, first_part, rows - first_part)
+
+    send_parts(0, 0)
+    all_of(need_all, n - 1, need_recv.at[0])
+    need_load = pltpu.make_async_copy(need_all, need_at, load_sem.at[2])
+    need_load.start()
+    need_load.wait()
+    send_near(source, 0)
+    send_near_parts(0)
+    plan_far()
+    plan_parts()
+
+    @pl.when(inner)
+    def _():
+        cross_y(0, 1)
+        relay(0, 0, True)
+        relay(0, 1, True)
+        cross_y(0, 0)
+
+    forward(0, x_now)
+    for s, here in enumerate((outer, inner)):
+        pl.when(here)(functools.partial(send_far, x_now, 1, s))
+    combine_near(0)
+    combine_far(0, False)
+    backward(1)
+    sent_parts(0)
+    send_parts(1, 1)
+    send_parts(1, 0)
+    send_near(x_now, 1)
+
+    @pl.when(outer)
+    def _():
+        send_near_parts(1)
+
+    @pl.when(inner)
+    def _():
+        relay(1, 0, False)
+        send_near_parts(1)
+        cross_y(1, 1)
+        relay(1, 1, False)
+        cross_y(1, 0)
+
+    forward(1, source_out)
+    combine_near(1)
+    combine_far(1, True)
+
+    all_of(need_all, n - 1, need_send.at[0])
+    all_of(x_far_out, cap, gate_send.at[1])
+    all_of(x_ins[0], half - 1, x_send.at[ITERS - 1])
+    sent_parts(ITERS - 1)
+
+    all_of(gates[0][0], rows, gate_send.at[0])
+
+    @pl.when(inner)
+    def _():
+        for s in range(2):
+            all_of(x_ins[0], half - 1, relay_send.at[2 * (ITERS - 1) + s])
+            all_of(y_cross_out.at[s], cap, y_cross_send.at[2 * (ITERS - 1) + s])
+
+
+def whole_exchange(source, target, tile_values, tile_rows, tile_peers, need_list, tile_count):
     n = lax.axis_size("rows")
     tiles_here, side, _ = tile_values.shape
     width = source.shape[1]
@@ -309,7 +826,7 @@
     vmem = pl.BlockSpec(memory_space=pltpu.VMEM)
     smem = pl.BlockSpec(memory_space=pltpu.SMEM)
     source_now, target_now = pl.pallas_call(
-        functools.partial(kernel, n, f_slots, b_slots),
+        functools.partial(general, n, f_slots, b_slots),
         out_shape=[pltpu.VMEM((rows,) + block, jnp.bfloat16)] * 2,
         in_specs=[smem] * 3 + [vmem] * 3 + [pl.BlockSpec(memory_space=pltpu.HBM)] * 3,
         out_specs=[vmem, vmem],
@@ -340,7 +857,7 @@
             pltpu.SemaphoreType.DMA((6,)),
         ],
         compiler_params=pltpu.CompilerParams(
-            collective_id=0, has_side_effects=True, vmem_limit_bytes=60000000
+            collective_id=1, has_side_effects=True, vmem_limit_bytes=65000000
         ),
     )(
         tile_rows,
@@ -354,6 +871,97 @@
         tile_values,
     )
     return source_now.reshape(-1, width), target_now.reshape(-1, width)
+
+
+def shards(source, target, tile_values, tile_rows, tile_peers, need_list, tile_count):
+    n = lax.axis_size("rows")
+    tiles_here, side, _ = tile_values.shape
+    width = source.shape[1]
+    rows = source.shape[0] // side
+    half, lanes = n // 2, lanes_for(n)
+    cap = min(rows, 13)
+    f_slots = slots_for(tiles_here, rows)
+    b_slots = slots_for(tiles_here, n)
+    tile_plan = (
+        lanes_for(2 * f_slots) + lanes_for(rows) + lanes_for(2 * b_slots) + lanes_for(n)
+    ) // 128
+    part_plan = 3 * (lanes_for(n) + lanes_for(rows)) // 128
+    far_plan = n + 2 * rows
+    block = (side, width)
+    vmem = pl.BlockSpec(memory_space=pltpu.VMEM)
+    smem = pl.BlockSpec(memory_space=pltpu.SMEM)
+    source_now, target_now, over = pl.pallas_call(
+        functools.partial(fast, n, cap, f_slots, b_slots),
+        out_shape=[pltpu.VMEM((rows,) + block, jnp.bfloat16)] * 2
+        + [jax.ShapeDtypeStruct((1, 1), jnp.int32)],
+        in_specs=[smem] * 3 + [vmem] * 3 + [pl.BlockSpec(memory_space=pltpu.HBM)] * 3,
+        out_specs=[vmem] * 3,
+        scratch_shapes=[
+            pltpu.VMEM((half,) + block, jnp.bfloat16),
+            pltpu.VMEM((cap,) + block, jnp.bfloat16),
+            [pltpu.VMEM((n,) + block, jnp.bfloat16)] * ITERS,
+            [[pltpu.VMEM((rows,) + block, jnp.bfloat16)] * 2] * ITERS,
+            pltpu.VMEM((2, half) + block, jnp.bfloat16),
+            pltpu.VMEM((n,) + block, jnp.bfloat16),
+            [pltpu.VMEM((half,) + block, jnp.bfloat16)] * ITERS,
+            [[pltpu.VMEM((half,) + block, jnp.bfloat16)] * 2] * ITERS,
+            pltpu.VMEM((2, cap) + block, jnp.bfloat16),
+            [pltpu.VMEM((cap + 1,) + block, jnp.bfloat16)] * ITERS,
+            pltpu.VMEM((rows,) + block, jnp.bfloat16),
+            pltpu.VMEM((rows,) + block, jnp.bfloat16),
+            pltpu.VMEM((rows,) + block, jnp.float32),
+            pltpu.VMEM((rows,) + block, jnp.float32),
+            pltpu.VMEM((f_slots + 1,) + block, jnp.float32),
+            pltpu.VMEM((b_slots + 1,) + block, jnp.bfloat16),
+            pltpu.VMEM((half + 1,) + block, jnp.float32),
+            pltpu.VMEM((rows,) + block, jnp.bfloat16),
+            pltpu.VMEM((rows,) + block, jnp.bfloat16),
+            pltpu.VMEM((tiles_here + 1, side, side), jnp.bfloat16),
+            pltpu.VMEM((1, lanes), jnp.int32),
+            pltpu.VMEM((n, 1, lanes), jnp.int32),
+            pltpu.SMEM((n, 1, lanes), jnp.int32),
+            pltpu.VMEM((tile_plan, 128), jnp.int32),
+            pltpu.SMEM((tile_plan, 128), jnp.int32),
+            pltpu.VMEM((part_plan, 128), jnp.int32),
+            pltpu.SMEM((part_plan, 128), jnp.int32),
+            pltpu.VMEM((far_plan, lanes), jnp.int32),
+            pltpu.SMEM((far_plan, lanes), jnp.int32),
+            pltpu.SemaphoreType.DMA((ITERS,)),
+            pltpu.SemaphoreType.DMA((ITERS,)),
+            pltpu.SemaphoreType.DMA((ITERS,)),
+            pltpu.SemaphoreType.DMA((2 * ITERS,)),
+            pltpu.SemaphoreType.DMA((2 * ITERS,)),
+            pltpu.SemaphoreType.DMA((ITERS,)),
+            pltpu.SemaphoreType.DMA((ITERS,)),
+            pltpu.SemaphoreType.DMA((2 * ITERS,)),
+            pltpu.SemaphoreType.DMA((2 * ITERS,)),
+            pltpu.SemaphoreType.DMA((ITERS,)),
+            pltpu.SemaphoreType.DMA((1,)),
+            pltpu.SemaphoreType.DMA((1,)),
+            pltpu.SemaphoreType.DMA((7,)),
+        ],
+        compiler_params=pltpu.CompilerParams(
+            collective_id=0, has_side_effects=True, vmem_limit_bytes=65000000
+        ),
+    )(
+        tile_rows,
+        tile_peers,
+        tile_count,
+        tile_rows.reshape(1, -1),
+        tile_peers.reshape(1, -1),
+        need_list,
+        source.reshape((rows,) + block),
+        target.reshape((rows,) + block),
+        tile_values,
+    )
+    source_now, target_now = source_now.reshape(-1, width), target_now.reshape(-1, width)
+    return lax.cond(
+        over.reshape(()) > 0,
+        lambda: whole_exchange(
+            source, target, tile_values, tile_rows, tile_peers, need_list, tile_count
+        ),
+        lambda: (source_now, target_now),
+    )
 
 
 def solution(mesh):

time: 108 us -> 102 us (0.944)
  the two profiles are of different devices: /device:TPU:13 before, /device:TPU:0 now
where the time goes in v2:
time: 102 us
  Pallas kernels  98.6 us (97%)
  between operations  2.1 us (2%)
  local copies, waits for them, and re-layouts  1.61 us (2%)
    pallas_call x1, Pallas kernels, shards(): pl.pallas_call(functools.partial(fast, n, cap, f_slots, b_slots), out_sha...  98.6 us

profile of v2, /device:TPU:0, one launch (start us, length us, event | category | flops | bytes accessed | tf_op | source)
XLA Modules:
  0.0 102.3 jit_solution(8136174935895483789)
XLA Ops:
  0.6 0.0 copy-start.2
  0.6 0.0 copy-start.1
  0.7 0.0 copy-start.3
  0.7 0.0 copy-start
  1.4 98.6 %shard_map.86 = (bf16[16,128,128]{2,1,0:T(8,128)(2,1)S(1)}, bf16[16,128,128]{2,1,0:T(8,128)(2,1)S(1)}, s32[1,1]{1,0:T(1,128)}) custom-call(s32[128]{0:T(128)} %row_of.1, s32[128]{0:T(128)} %peer_of.1, s32[1]{0:T(128)S(6)} %copy.19.live_count, s32[1,128]{1,0:T(1,128)} %bitcast.21, s32[1,128]{1,0:T(1,128)} %bitcast.23, s32[1,32]{1,0:T(1,128)} %need.1, ...), custom_call_target="tpu_custom_call" | custom-call | tf_op jit(solution)/shard_map/pallas_call | solution.py:893
  100.6 0.0 copy-done.2
  100.6 0.0 copy-done.1
  100.6 0.0 copy-done.3
  100.7 0.0 copy-done
  100.7 0.8 copy.17
  101.5 0.8 copy.18
  (1 shorter events, 0.0 us)
Async XLA Ops:
  0.6 100.0 %copy-start.2 = (s32[128]{0:T(128)S(1)}, s32[128]{0:T(128)}, u32[]{:S(2)}) copy-start(s32[128]{0:T(128)} %peer_of.1) | copy-start | bytes 1540
  0.6 100.0 %copy-start.1 = (s32[128]{0:T(128)S(1)}, s32[128]{0:T(128)}, u32[]{:S(2)}) copy-start(s32[128]{0:T(128)} %row_of.1) | copy-start | bytes 1540
  0.7 100.0 %copy-start.3 = (s32[1,32]{1,0:T(1,128)S(1)}, s32[1,32]{1,0:T(1,128)}, u32[]{:S(2)}) copy-start(s32[1,32]{1,0:T(1,128)} %need.1) | copy-start | bytes 388
  0.7 100.0 %copy-start = (bf16[2048,128]{1,0:T(8,128)(2,1)S(1)}, bf16[2048,128]{1,0:T(8,128)(2,1)}, u32[]{:S(2)}) copy-start(bf16[2048,128]{1,0:T(8,128)(2,1)} %param.9) | copy-start | bytes 1572868

commit v3 on v2

--- a/solution.py
+++ b/solution.py
@@ -321,6 +321,8 @@
     x_near_out,
     x_far_out,
     x_ins,
+    hubs,
+    hub_out,
     gates,
     relay_out,
     y_out,
@@ -349,6 +351,9 @@
     far_at,
     x_send,
     x_recv,
+    hub_send,
+    hub_recv,
+    spoke_send,
     gate_send,
     gate_recv,
     relay_send,
@@ -373,6 +378,10 @@
     outer = jnp.logical_not(inner)
     far_gate = (2 - upper) * plane + column
     near_gates = (1 + upper) * plane
+    mine_first = me - column
+    other_first = 2 * near_first + plane - mine_first
+    near_gate = near_gates + column
+    outer_owner = 3 * upper * plane + column
     far_planes = (3 * (1 - upper) * plane, (2 - upper) * plane)
     far_owner = tuple(first + column for first in far_planes)
     f_seat, f_last = 0, lanes_for(2 * f_slots) // 128
@@ -453,15 +462,6 @@
         return carry
 
     lax.fori_loop(1, n, ask, 0)
-
-    def send_whole(s, first, count):
-        push(
-            source.at[pl.ds(first, count)],
-            gates[0][s].at[pl.ds(first, count)],
-            gate_send.at[0],
-            gate_recv.at[s],
-            far_gate,
-        )
 
     def needs():
         return need_all[...].reshape(n, lanes).astype(jnp.float32)
@@ -529,33 +529,90 @@
     def asked(d):
         return jnp.clip(need_at[d, 0, me], 0, rows - 1)
 
+    def to_plane(one, first, low):
+        def step(k, carry):
+            one(first + lax.rem(column + k, plane), plane + k if low else k)
+            return carry
+
+        lax.fori_loop(low, plane, step, 0)
+
+    def to_half(one):
+        to_plane(one, other_first, 0)
+        to_plane(one, mine_first, 1)
+
     def send_near(blocks, it):
         x_in = x_ins[it]
-        if it:
-            all_of(x_in, half - 1, x_send.at[it - 1])
-
-        def one(k, carry):
-            peer = near_first + lax.rem(spot + k, half)
+
+        def one(peer, k):
             x_near_out[k] = blocks[asked(peer)]
             push(x_near_out.at[k], x_in.at[me], x_send.at[it], x_recv.at[it], peer)
-            return carry
-
-        lax.fori_loop(1, half, one, 0)
+
+        if it:
+            sent_near(it - 1)
+
+        @pl.when(inner)
+        def _():
+            to_half(one)
+
+        @pl.when(outer)
+        def _():
+            to_plane(one, mine_first, 1)
+
         x_in[me] = blocks[asked(me)]
 
-    def send_far(blocks, it, s):
+    def sent_near(it):
+        @pl.when(inner)
+        def _():
+            all_of(x_near_out, half - 1, x_send.at[it])
+
+        @pl.when(outer)
+        def _():
+            all_of(x_near_out, plane - 1, x_send.at[it])
+
+    def send_hub(blocks, it):
+        push(blocks, hubs[it], hub_send.at[it], hub_recv.at[it], near_gate)
+
+    def send_far(blocks, it, s, owner):
+        if it:
+            sent_far(it - 1, s)
+
         def one(i, carry):
-            x_far_out[i] = blocks[jnp.clip(far_at[far_list + i, me], 0, rows - 1)]
+            x_far_out[s, i] = blocks[jnp.clip(far_at[far_list + i, owner], 0, rows - 1)]
             return carry
 
         lax.fori_loop(0, cap, one, 0)
         push(
-            x_far_out,
+            x_far_out.at[s],
             gates[it][s].at[pl.ds(0, cap)],
-            gate_send.at[it],
+            gate_send.at[2 * it + s],
             gate_recv.at[2 * it + s],
             far_gate,
         )
+
+    def sent_far(it, s):
+        whole = it == 0 and s == 1
+        all_of(gates[it][s], rows if whole else cap, gate_send.at[2 * it + s])
+
+    def hub(it):
+        held, x_in = hubs[it], x_ins[it]
+        all_of(held, rows, hub_recv.at[it])
+        send_far(held, it, 0, outer_owner)
+        if it:
+            all_of(hub_out, plane - 1, spoke_send.at[it - 1])
+
+        def block(d):
+            return held[jnp.clip(need_at[d, 0, outer_owner], 0, rows - 1)]
+
+        def one(k, carry):
+            peer = near_gates + lax.rem(column + k, plane)
+            hub_out[k] = block(peer)
+            push(
+                hub_out.at[k], x_in.at[outer_owner], spoke_send.at[it], x_recv.at[it], peer
+            )
+            return carry
+
+        lax.fori_loop(1, plane, one, 0)
+        x_in[outer_owner] = block(me)
 
     def relay(it, s, whole):
         gate, x_in, owner = gates[it][s], x_ins[it], far_owner[s]
@@ -567,8 +624,7 @@
             at = need_at[d, 0, owner] if whole else far_at[d, owner]
             return gate[jnp.clip(at, 0, (rows if whole else cap) - 1)]
 
-        def one(k, carry):
-            peer = near_first + lax.rem(spot + k, half)
+        def one(peer, k):
             relay_out[s, k] = block(peer)
             push(
                 relay_out.at[s, k],
@@ -577,9 +633,8 @@
                 x_recv.at[it],
                 peer,
             )
-            return carry
-
-        lax.fori_loop(1, half, one, 0)
+
+        to_half(one)
         x_in[owner] = block(me)
 
     def backward(it):
@@ -626,13 +681,11 @@
         lax.fori_loop(1, plane, one, 0)
 
     def send_near_parts(it):
-        def one(k, carry):
-            peer = near_first + lax.rem(spot + k, half)
+        def one(peer, k):
             y_out[peer] = part(peer)
             push(y_out.at[peer], y_near_ins[it].at[spot], y_send.at[it], y_near_recv.at[it], peer)
-            return carry
-
-        lax.fori_loop(1, half, one, 0)
+
+        to_half(one)
         y_near_ins[it][spot] = part(me)
 
     def sent_parts(it):
@@ -649,7 +702,7 @@
 
         @pl.when(inner)
         def _():
-            all_of(x_in, n - 3, x_recv.at[it])
+            all_of(x_in, n - 4, x_recv.at[it])
 
         @pl.when(outer)
         def _():
@@ -735,62 +788,64 @@
 
         lax.fori_loop(0, rows, settle, 0)
 
-    first_part = 5 * rows // 8
+    def learn_needs():
+        all_of(need_all, n - 1, need_recv.at[0])
+        need_load = pltpu.make_async_copy(need_all, need_at, load_sem.at[2])
+        need_load.start()
+        plan_far()
+        need_load.wait()
+
+    @pl.when(inner)
+    def _():
+        push(source, gates[0][1], gate_send.at[1], gate_recv.at[1], far_gate)
 
     @pl.when(outer)
     def _():
-        send_whole(0, 0, first_part)
-
-    @pl.when(inner)
-    def _():
-        send_whole(1, 0, rows)
+        send_hub(source, 0)
 
     tile_load.wait()
     backward(0)
     send_parts(0, 1)
+    send_parts(0, 0)
+    learn_needs()
+    send_near(source, 0)
+    pl.when(outer)(functools.partial(send_near_parts, 0))
+    plan_parts()
+
+    @pl.when(inner)
+    def _():
+        hub(0)
+        relay(0, 1, True)
+        cross_y(0, 1)
+        relay(0, 0, False)
+        send_near_parts(0)
+        cross_y(0, 0)
+
+    forward(0, x_now)
+
+    @pl.when(inner)
+    def _():
+        send_far(x_now, 1, 1, me)
 
     @pl.when(outer)
     def _():
-        send_whole(0, first_part, rows - first_part)
-
-    send_parts(0, 0)
-    all_of(need_all, n - 1, need_recv.at[0])
-    need_load = pltpu.make_async_copy(need_all, need_at, load_sem.at[2])
-    need_load.start()
-    need_load.wait()
-    send_near(source, 0)
-    send_near_parts(0)
-    plan_far()
-    plan_parts()
-
-    @pl.when(inner)
-    def _():
-        cross_y(0, 1)
-        relay(0, 0, True)
-        relay(0, 1, True)
-        cross_y(0, 0)
-
-    forward(0, x_now)
-    for s, here in enumerate((outer, inner)):
-        pl.when(here)(functools.partial(send_far, x_now, 1, s))
+        send_hub(x_now, 1)
+
+    send_near(x_now, 1)
     combine_near(0)
     combine_far(0, False)
     backward(1)
     sent_parts(0)
     send_parts(1, 1)
     send_parts(1, 0)
-    send_near(x_now, 1)
-
-    @pl.when(outer)
-    def _():
-        send_near_parts(1)
+    send_near_parts(1)
 
     @pl.when(inner)
     def _():
+        relay(1, 1, False)
+        hub(1)
+        cross_y(1, 1)
         relay(1, 0, False)
-        send_near_parts(1)
-        cross_y(1, 1)
-        relay(1, 1, False)
         cross_y(1, 0)
 
     forward(1, source_out)
@@ -798,15 +853,19 @@
     combine_far(1, True)
 
     all_of(need_all, n - 1, need_send.at[0])
-    all_of(x_far_out, cap, gate_send.at[1])
-    all_of(x_ins[0], half - 1, x_send.at[ITERS - 1])
+    sent_near(ITERS - 1)
     sent_parts(ITERS - 1)
 
-    all_of(gates[0][0], rows, gate_send.at[0])
+    @pl.when(outer)
+    def _():
+        for it in range(ITERS):
+            all_of(hubs[it], rows, hub_send.at[it])
 
     @pl.when(inner)
     def _():
+        all_of(hub_out, plane - 1, spoke_send.at[ITERS - 1])
         for s in range(2):
+            sent_far(ITERS - 1, s)
             all_of(x_ins[0], half - 1, relay_send.at[2 * (ITERS - 1) + s])
             all_of(y_cross_out.at[s], cap, y_cross_send.at[2 * (ITERS - 1) + s])
 
@@ -898,8 +957,10 @@
         out_specs=[vmem] * 3,
         scratch_shapes=[
             pltpu.VMEM((half,) + block, jnp.bfloat16),
-            pltpu.VMEM((cap,) + block, jnp.bfloat16),
+            pltpu.VMEM((2, cap) + block, jnp.bfloat16),
             [pltpu.VMEM((n,) + block, jnp.bfloat16)] * ITERS,
+            [pltpu.VMEM((rows,) + block, jnp.bfloat16)] * ITERS,
+            pltpu.VMEM((n // 4,) + block, jnp.bfloat16),
             [[pltpu.VMEM((rows,) + block, jnp.bfloat16)] * 2] * ITERS,
             pltpu.VMEM((2, half) + block, jnp.bfloat16),
             pltpu.VMEM((n,) + block, jnp.bfloat16),
@@ -929,6 +990,9 @@
             pltpu.SemaphoreType.DMA((ITERS,)),
             pltpu.SemaphoreType.DMA((ITERS,)),
             pltpu.SemaphoreType.DMA((ITERS,)),
+            pltpu.SemaphoreType.DMA((ITERS,)),
+            pltpu.SemaphoreType.DMA((ITERS,)),
+            pltpu.SemaphoreType.DMA((2 * ITERS,)),
             pltpu.SemaphoreType.DMA((2 * ITERS,)),
             pltpu.SemaphoreType.DMA((2 * ITERS,)),
             pltpu.SemaphoreType.DMA((ITERS,)),

time: 102 us -> 97.3 us (0.954)
  Pallas kernels: 98.6 us -> 93.4 us
    pallas_call x1, Pallas kernels: 98.6 us -> 93.4 us  [shards(): pl.pallas_call(functools.partial(fast, n, cap, f_slots, b_slots), out_sha...]
where the time goes in v3:
time: 97.3 us; the launch traced here: 97.1 us
  Pallas kernels  93.4 us (96%)
  between operations  2.1 us (2%)
  local copies, waits for them, and re-layouts  1.61 us (2%)
    pallas_call x1, Pallas kernels, shards(): pl.pallas_call(functools.partial(fast, n, cap, f_slots, b_slots), out_sha...  93.4 us

profile of v3, /device:TPU:0, one launch (start us, length us, event | category | flops | bytes accessed | tf_op | source)
XLA Modules:
  0.0 97.1 jit_solution(8237932101151156812)
XLA Ops:
  0.6 0.0 copy-start.2
  0.6 0.0 copy-start.1
  0.7 0.0 copy-start.3
  0.7 0.0 copy-start
  1.4 93.4 %shard_map.86 = (bf16[16,128,128]{2,1,0:T(8,128)(2,1)S(1)}, bf16[16,128,128]{2,1,0:T(8,128)(2,1)S(1)}, s32[1,1]{1,0:T(1,128)}) custom-call(s32[128]{0:T(128)} %row_of.1, s32[128]{0:T(128)} %peer_of.1, s32[1]{0:T(128)S(6)} %copy.19.live_count, s32[1,128]{1,0:T(1,128)} %bitcast.21, s32[1,128]{1,0:T(1,128)} %bitcast.23, s32[1,32]{1,0:T(1,128)} %need.1, ...), custom_call_target="tpu_custom_call" | custom-call | tf_op jit(solution)/shard_map/pallas_call | solution.py:952
  95.4 0.0 copy-done.2
  95.5 0.0 copy-done.1
  95.5 0.0 copy-done.3
  95.5 0.0 copy-done
  95.5 0.8 copy.17
  96.3 0.8 copy.18
  (1 shorter events, 0.0 us)
Async XLA Ops:
  0.6 94.8 %copy-start.2 = (s32[128]{0:T(128)S(1)}, s32[128]{0:T(128)}, u32[]{:S(2)}) copy-start(s32[128]{0:T(128)} %peer_of.1) | copy-start | bytes 1540
  0.6 94.8 %copy-start.1 = (s32[128]{0:T(128)S(1)}, s32[128]{0:T(128)}, u32[]{:S(2)}) copy-start(s32[128]{0:T(128)} %row_of.1) | copy-start | bytes 1540
  0.7 94.8 %copy-start.3 = (s32[1,32]{1,0:T(1,128)S(1)}, s32[1,32]{1,0:T(1,128)}, u32[]{:S(2)}) copy-start(s32[1,32]{1,0:T(1,128)} %need.1) | copy-start | bytes 388
  0.7 94.8 %copy-start = (bf16[2048,128]{1,0:T(8,128)(2,1)S(1)}, bf16[2048,128]{1,0:T(8,128)(2,1)}, u32[]{:S(2)}) copy-start(bf16[2048,128]{1,0:T(8,128)(2,1)} %param.9) | copy-start | bytes 1572868

commit v4 on v3

--- a/solution.py
+++ b/solution.py
@@ -536,9 +536,10 @@
 
         lax.fori_loop(low, plane, step, 0)
 
-    def to_half(one):
-        to_plane(one, other_first, 0)
-        to_plane(one, mine_first, 1)
+    def to_half(one, mine_ahead=False):
+        legs = (other_first, 0), (mine_first, 1)
+        for first, low in legs[::-1] if mine_ahead else legs:
+            to_plane(one, first, low)
 
     def send_near(blocks, it):
         x_in = x_ins[it]
@@ -556,6 +557,8 @@
 
         @pl.when(outer)
         def _():
+            if it:
+                to_plane(one, other_first, 0)
             to_plane(one, mine_first, 1)
 
         x_in[me] = blocks[asked(me)]
@@ -567,38 +570,68 @@
 
         @pl.when(outer)
         def _():
-            all_of(x_near_out, plane - 1, x_send.at[it])
-
-    def send_hub(blocks, it):
-        push(blocks, hubs[it], hub_send.at[it], hub_recv.at[it], near_gate)
-
-    def send_far(blocks, it, s, owner):
-        if it:
-            sent_far(it - 1, s)
-
+            all_of(x_near_out, half - 1 if it else plane - 1, x_send.at[it])
+
+    def pack_far(blocks, s, owner):
         def one(i, carry):
             x_far_out[s, i] = blocks[jnp.clip(far_at[far_list + i, owner], 0, rows - 1)]
             return carry
 
         lax.fori_loop(0, cap, one, 0)
+
+    first_part = rows // 2
+    hub_parts = (0, first_part, 0), (first_part, rows - first_part, ITERS)
+
+    def send_hub_whole():
+        for first, count, sem in hub_parts:
+            piece = pl.ds(first, count)
+            push(
+                source.at[piece], hubs[0].at[piece], hub_send.at[0], hub_recv.at[sem], near_gate
+            )
+
+    def cross_hub_whole(half_at):
+        first, count, sem = hub_parts[half_at]
+        piece = pl.ds(first, count)
+        all_of(hubs[0], count, hub_recv.at[sem])
         push(
-            x_far_out.at[s],
-            gates[it][s].at[pl.ds(0, cap)],
-            gate_send.at[2 * it + s],
-            gate_recv.at[2 * it + s],
+            hubs[0].at[piece], gates[0][0].at[piece], gate_send.at[0], gate_recv.at[0], far_gate
+        )
+
+    def send_hub_packed():
+        pack_far(x_now, 0, me)
+        push(
+            x_far_out.at[0],
+            hubs[1].at[pl.ds(0, cap)],
+            hub_send.at[1],
+            hub_recv.at[1],
+            near_gate,
+        )
+
+    def cross_hub_packed():
+        all_of(hubs[1], cap, hub_recv.at[1])
+        push(
+            hubs[1].at[pl.ds(0, cap)],
+            gates[1][0].at[pl.ds(0, cap)],
+            gate_send.at[2],
+            gate_recv.at[2],
             far_gate,
         )
 
+    def send_far():
+        pack_far(x_now, 1, me)
+        push(
+            x_far_out.at[1],
+            gates[1][1].at[pl.ds(0, cap)],
+            gate_send.at[3],
+            gate_recv.at[3],
+            far_gate,
+        )
+
     def sent_far(it, s):
-        whole = it == 0 and s == 1
-        all_of(gates[it][s], rows if whole else cap, gate_send.at[2 * it + s])
-
-    def hub(it):
-        held, x_in = hubs[it], x_ins[it]
-        all_of(held, rows, hub_recv.at[it])
-        send_far(held, it, 0, outer_owner)
-        if it:
-            all_of(hub_out, plane - 1, spoke_send.at[it - 1])
+        all_of(gates[it][s], cap if it else rows, gate_send.at[2 * it + s])
+
+    def serve_hub():
+        held, x_in = hubs[0], x_ins[0]
 
         def block(d):
             return held[jnp.clip(need_at[d, 0, outer_owner], 0, rows - 1)]
@@ -607,7 +640,7 @@
             peer = near_gates + lax.rem(column + k, plane)
             hub_out[k] = block(peer)
             push(
-                hub_out.at[k], x_in.at[outer_owner], spoke_send.at[it], x_recv.at[it], peer
+                hub_out.at[k], x_in.at[outer_owner], spoke_send.at[0], x_recv.at[0], peer
             )
             return carry
 
@@ -634,7 +667,7 @@
                 peer,
             )
 
-        to_half(one)
+        to_half(one, it)
         x_in[owner] = block(me)
 
     def backward(it):
@@ -702,7 +735,7 @@
 
         @pl.when(inner)
         def _():
-            all_of(x_in, n - 4, x_recv.at[it])
+            all_of(x_in, n - 3 if it else n - 4, x_recv.at[it])
 
         @pl.when(outer)
         def _():
@@ -750,7 +783,7 @@
 
         def one(i, carry):
             total = c_sums[seat(part_at, first + c_last, i, half)]
-            y_cross_out[s, i] = total.astype(jnp.bfloat16)
+            y_cross_out[s, i] = (total.T if it == ITERS - 1 else total).astype(jnp.bfloat16)
             return carry
 
         lax.fori_loop(0, cap, one, 0)
@@ -767,7 +800,8 @@
         gather(y_near_ins[it], 0, asked)
 
         def settle(b, carry):
-            y_mid[b] = y_base[b] + c_sums[seat(part_at, c_last, b, half)]
+            total = y_base[b] + c_sums[seat(part_at, c_last, b, half)]
+            y_mid[b] = total.T if it == ITERS - 1 else total
             return carry
 
         lax.fori_loop(0, rows, settle, 0)
@@ -779,11 +813,9 @@
         def settle(b, carry):
             at = jnp.clip(far_at[far_slot + b, me], 0, cap)
             total = y_mid[b] + y_far[at].astype(jnp.float32)
-            scale = lax.rsqrt(jnp.mean(total * total, axis=0, keepdims=True) + epsilon)
-            if final:
-                target_out[b] = (total * scale).T.astype(jnp.bfloat16)
-            else:
-                y_now[b] = (total * scale).astype(jnp.bfloat16)
+            over = -1 if final else 0
+            scale = lax.rsqrt(jnp.mean(total * total, axis=over, keepdims=True) + epsilon)
+            (target_out if final else y_now)[b] = (total * scale).astype(jnp.bfloat16)
             return carry
 
         lax.fori_loop(0, rows, settle, 0)
@@ -801,7 +833,7 @@
 
     @pl.when(outer)
     def _():
-        send_hub(source, 0)
+        send_hub_whole()
 
     tile_load.wait()
     backward(0)
@@ -809,41 +841,44 @@
     send_parts(0, 0)
     learn_needs()
     send_near(source, 0)
+    pl.when(inner)(functools.partial(cross_hub_whole, 0))
     pl.when(outer)(functools.partial(send_near_parts, 0))
     plan_parts()
 
     @pl.when(inner)
     def _():
-        hub(0)
+        cross_hub_whole(1)
+        serve_hub()
         relay(0, 1, True)
+        send_near_parts(0)
         cross_y(0, 1)
-        relay(0, 0, False)
-        send_near_parts(0)
+        relay(0, 0, True)
         cross_y(0, 0)
 
     forward(0, x_now)
 
     @pl.when(inner)
     def _():
-        send_far(x_now, 1, 1, me)
+        send_far()
 
     @pl.when(outer)
     def _():
-        send_hub(x_now, 1)
-
-    send_near(x_now, 1)
+        send_hub_packed()
+
+    pl.when(inner)(functools.partial(send_near, x_now, 1))
     combine_near(0)
     combine_far(0, False)
     backward(1)
     sent_parts(0)
     send_parts(1, 1)
     send_parts(1, 0)
+    pl.when(outer)(functools.partial(send_near, x_now, 1))
     send_near_parts(1)
 
     @pl.when(inner)
     def _():
         relay(1, 1, False)
-        hub(1)
+        cross_hub_packed()
         cross_y(1, 1)
         relay(1, 0, False)
         cross_y(1, 0)
@@ -859,13 +894,14 @@
     @pl.when(outer)
     def _():
         for it in range(ITERS):
-            all_of(hubs[it], rows, hub_send.at[it])
+            all_of(hubs[it], cap if it else rows, hub_send.at[it])
 
     @pl.when(inner)
     def _():
-        all_of(hub_out, plane - 1, spoke_send.at[ITERS - 1])
+        all_of(hub_out, plane - 1, spoke_send.at[0])
         for s in range(2):
-            sent_far(ITERS - 1, s)
+            sent_far(0, s)
+            sent_far(1, s)
             all_of(x_ins[0], half - 1, relay_send.at[2 * (ITERS - 1) + s])
             all_of(y_cross_out.at[s], cap, y_cross_send.at[2 * (ITERS - 1) + s])
 
@@ -990,7 +1026,7 @@
             pltpu.SemaphoreType.DMA((ITERS,)),
             pltpu.SemaphoreType.DMA((ITERS,)),
             pltpu.SemaphoreType.DMA((ITERS,)),
-            pltpu.SemaphoreType.DMA((ITERS,)),
+            pltpu.SemaphoreType.DMA((ITERS + 1,)),
             pltpu.SemaphoreType.DMA((ITERS,)),
             pltpu.SemaphoreType.DMA((2 * ITERS,)),
             pltpu.SemaphoreType.DMA((2 * ITERS,)),

time: 97.3 us -> 96.1 us (0.988)
  Pallas kernels: 93.4 us -> 92.3 us
    pallas_call x1, Pallas kernels: 93.4 us -> 92.3 us  [shards(): pl.pallas_call(functools.partial(fast, n, cap, f_slots, b_slots), out_sha...]
where the time goes in v4:
time: 96.1 us; the launch traced here: 96 us
  Pallas kernels  92.3 us (96%)
  between operations  2.1 us (2%)
  local copies, waits for them, and re-layouts  1.61 us (2%)
    pallas_call x1, Pallas kernels, shards(): pl.pallas_call(functools.partial(fast, n, cap, f_slots, b_slots), out_sha...  92.3 us

profile of v4, /device:TPU:0, one launch (start us, length us, event | category | flops | bytes accessed | tf_op | source)
XLA Modules:
  0.0 96.0 jit_solution(5463123273951445876)
XLA Ops:
  0.6 0.0 copy-start.2
  0.6 0.0 copy-start.1
  0.7 0.0 copy-start.3
  0.7 0.0 copy-start
  1.4 92.3 %shard_map.86 = (bf16[16,128,128]{2,1,0:T(8,128)(2,1)S(1)}, bf16[16,128,128]{2,1,0:T(8,128)(2,1)S(1)}, s32[1,1]{1,0:T(1,128)}) custom-call(s32[128]{0:T(128)} %row_of.1, s32[128]{0:T(128)} %peer_of.1, s32[1]{0:T(128)S(6)} %copy.19.live_count, s32[1,128]{1,0:T(1,128)} %bitcast.21, s32[1,128]{1,0:T(1,128)} %bitcast.23, s32[1,32]{1,0:T(1,128)} %need.1, ...), custom_call_target="tpu_custom_call" | custom-call | tf_op jit(solution)/shard_map/pallas_call | solution.py:988
  94.3 0.0 copy-done.2
  94.3 0.0 copy-done.1
  94.4 0.0 copy-done.3
  94.4 0.0 copy-done
  94.4 0.8 copy.17
  95.2 0.8 copy.18
  (1 shorter events, 0.0 us)
Async XLA Ops:
  0.6 93.7 %copy-start.2 = (s32[128]{0:T(128)S(1)}, s32[128]{0:T(128)}, u32[]{:S(2)}) copy-start(s32[128]{0:T(128)} %peer_of.1) | copy-start | bytes 1540
  0.6 93.7 %copy-start.1 = (s32[128]{0:T(128)S(1)}, s32[128]{0:T(128)}, u32[]{:S(2)}) copy-start(s32[128]{0:T(128)} %row_of.1) | copy-start | bytes 1540
  0.7 93.7 %copy-start.3 = (s32[1,32]{1,0:T(1,128)S(1)}, s32[1,32]{1,0:T(1,128)}, u32[]{:S(2)}) copy-start(s32[1,32]{1,0:T(1,128)} %need.1) | copy-start | bytes 388
  0.7 93.7 %copy-start = (bf16[2048,128]{1,0:T(8,128)(2,1)S(1)}, bf16[2048,128]{1,0:T(8,128)(2,1)}, u32[]{:S(2)}) copy-start(bf16[2048,128]{1,0:T(8,128)(2,1)} %param.9) | copy-start | bytes 1572868

commit v5 on v4

--- a/solution.py
+++ b/solution.py
@@ -349,6 +349,7 @@
     part_at,
     far_plan,
     far_at,
+    over,
     x_send,
     x_recv,
     hub_send,
@@ -487,7 +488,8 @@
         far_plan[pl.ds(0, n), :] = place.astype(jnp.int32)
         far_plan[pl.ds(far_list, rows), :] = listed.astype(jnp.int32)
         worst = jnp.max(before, axis=1, keepdims=True)
-        over_out[...] = (worst > cap).astype(jnp.int32)
+        over[...] = (worst > cap).astype(jnp.int32)
+        pltpu.make_async_copy(over, over_out, load_sem.at[7]).start()
         load = pltpu.make_async_copy(far_plan, far_at, load_sem.at[6])
         load.start()
         load.wait()
@@ -888,6 +890,7 @@
     combine_far(1, True)
 
     all_of(need_all, n - 1, need_send.at[0])
+    pltpu.make_async_copy(over, over_out, load_sem.at[7]).wait()
     sent_near(ITERS - 1)
     sent_parts(ITERS - 1)
 
@@ -990,7 +993,7 @@
         out_shape=[pltpu.VMEM((rows,) + block, jnp.bfloat16)] * 2
         + [jax.ShapeDtypeStruct((1, 1), jnp.int32)],
         in_specs=[smem] * 3 + [vmem] * 3 + [pl.BlockSpec(memory_space=pltpu.HBM)] * 3,
-        out_specs=[vmem] * 3,
+        out_specs=[vmem] * 2 + [pl.BlockSpec(memory_space=pltpu.HBM)],
         scratch_shapes=[
             pltpu.VMEM((half,) + block, jnp.bfloat16),
             pltpu.VMEM((2, cap) + block, jnp.bfloat16),
@@ -1023,6 +1026,7 @@
             pltpu.SMEM((part_plan, 128), jnp.int32),
             pltpu.VMEM((far_plan, lanes), jnp.int32),
             pltpu.SMEM((far_plan, lanes), jnp.int32),
+            pltpu.VMEM((1, 1), jnp.int32),
             pltpu.SemaphoreType.DMA((ITERS,)),
             pltpu.SemaphoreType.DMA((ITERS,)),
             pltpu.SemaphoreType.DMA((ITERS,)),
@@ -1038,7 +1042,7 @@
             pltpu.SemaphoreType.DMA((ITERS,)),
             pltpu.SemaphoreType.DMA((1,)),
             pltpu.SemaphoreType.DMA((1,)),
-            pltpu.SemaphoreType.DMA((7,)),
+            pltpu.SemaphoreType.DMA((8,)),
         ],
         compiler_params=pltpu.CompilerParams(
             collective_id=0, has_side_effects=True, vmem_limit_bytes=65000000

time: 96.1 us -> 95.6 us (level)
  no operation moved by 1% of the time
where the time goes in v5:
time: 95.6 us; the launch traced here: 95.4 us
  Pallas kernels  91.7 us (96%)
  between operations  2.1 us (2%)
  local copies, waits for them, and re-layouts  1.61 us (2%)
    pallas_call x1, Pallas kernels, shards(): pl.pallas_call(functools.partial(fast, n, cap, f_slots, b_slots), out_sha...  91.7 us

profile of v5, /device:TPU:0, one launch (start us, length us, event | category | flops | bytes accessed | tf_op | source)
XLA Modules:
  0.0 95.4 jit_solution(10491001321434945220)
XLA Ops:
  0.6 0.0 copy-start.2
  0.6 0.0 copy-start.1
  0.7 0.0 copy-start.3
  0.7 0.0 copy-start
  1.4 91.7 %shard_map.86 = (bf16[16,128,128]{2,1,0:T(8,128)(2,1)S(1)}, bf16[16,128,128]{2,1,0:T(8,128)(2,1)S(1)}, s32[1,1]{1,0:T(1,128)}) custom-call(s32[128]{0:T(128)} %row_of.1, s32[128]{0:T(128)} %peer_of.1, s32[1]{0:T(128)S(6)} %copy.19.live_count, s32[1,128]{1,0:T(1,128)} %bitcast.21, s32[1,128]{1,0:T(1,128)} %bitcast.23, s32[1,32]{1,0:T(1,128)} %need.1, ...), custom_call_target="tpu_custom_call" | custom-call | tf_op jit(solution)/shard_map/pallas_call | solution.py:991
  93.8 0.0 copy-done.2
  93.8 0.0 copy-done.1
  93.8 0.0 copy-done.3
  93.8 0.0 copy-done
  93.8 0.8 copy.17
  94.6 0.8 copy.18
  (1 shorter events, 0.0 us)
Async XLA Ops:
  0.6 93.1 %copy-start.2 = (s32[128]{0:T(128)S(1)}, s32[128]{0:T(128)}, u32[]{:S(2)}) copy-start(s32[128]{0:T(128)} %peer_of.1) | copy-start | bytes 1540
  0.6 93.1 %copy-start.1 = (s32[128]{0:T(128)S(1)}, s32[128]{0:T(128)}, u32[]{:S(2)}) copy-start(s32[128]{0:T(128)} %row_of.1) | copy-start | bytes 1540
  0.7 93.1 %copy-start.3 = (s32[1,32]{1,0:T(1,128)S(1)}, s32[1,32]{1,0:T(1,128)}, u32[]{:S(2)}) copy-start(s32[1,32]{1,0:T(1,128)} %need.1) | copy-start | bytes 388
  0.7 93.1 %copy-start = (bf16[2048,128]{1,0:T(8,128)(2,1)S(1)}, bf16[2048,128]{1,0:T(8,128)(2,1)}, u32[]{:S(2)}) copy-start(bf16[2048,128]{1,0:T(8,128)(2,1)} %param.9) | copy-start | bytes 1572868
